TPU v7x, 32 devices: a whole 2x2x4 slice. The times are simulated.
32 devices in a mesh: rows: 4 (over z), width: 4 (over y, x), site: 2 (over core).
Axes of the slice: x: 2, y: 2, z: 4, core: 2. Of those that a mesh axis runs over, the one named last changes fastest.
Arguments:
- weight_query: float32 [8192, 4096], P(('site', 'rows'), 'width'), parts along dimension 0, may hold values from -0.125 to 0.125
- moment_query: float32 [8192, 4096], P(('site', 'rows'), 'width'), parts along dimension 0, may hold values from -6 to 6
- square_query: float32 [8192, 4096], P(('site', 'rows'), 'width'), parts along dimension 0, may hold values from 0.1 to 10
- weight_key: float32 [8192, 1024], P(('site', 'rows'), 'width'), parts along dimension 0, may hold values from -0.125 to 0.125
- moment_key: float32 [8192, 1024], P(('site', 'rows'), 'width'), parts along dimension 0, may hold values from -6 to 6
- square_key: float32 [8192, 1024], P(('site', 'rows'), 'width'), parts along dimension 0, may hold values from 0.1 to 10
- weight_value: float32 [8192, 1024], P(('site', 'rows'), 'width'), parts along dimension 0, may hold values from -0.125 to 0.125
- moment_value: float32 [8192, 1024], P(('site', 'rows'), 'width'), parts along dimension 0, may hold values from -6 to 6
- square_value: float32 [8192, 1024], P(('site', 'rows'), 'width'), parts along dimension 0, may hold values from 0.1 to 10
- norm_train: float32 [8192], P(('site', 'rows', 'width')), parts along dimension 0, may hold values from 0.25 to 1.75
- norm_step: float32 [8192], P(('site', 'rows', 'width')), parts along dimension 0, may hold values from -0.3 to 0.3
Outputs:
- final_query: bfloat16 [8192, 4096], P('site', 'width'), parts along dimension 0
- final_key: bfloat16 [8192, 1024], P('site', 'width'), parts along dimension 0
- final_value: bfloat16 [8192, 1024], P('site', 'width'), parts along dimension 0
- column_query: float32 [8192], P(('site', 'width')), parts along dimension 0
- column_key: float32 [2048], P(('site', 'width')), parts along dimension 0
- column_value: float32 [2048], P(('site', 'width')), parts along dimension 0
- serve_norm: bfloat16 [8192], P('site'), parts along dimension 0
- result_query: float32 [8192, 4096], P(('site', 'rows'), 'width'), parts along dimension 0
- result_key: float32 [8192, 1024], P(('site', 'rows'), 'width'), parts along dimension 0
- result_value: float32 [8192, 1024], P(('site', 'rows'), 'width'), parts along dimension 0
There are 2 independent parts, one for each index of `site`. A program takes and returns all parts, laid end to end along the dimension named above; each array names one. Nothing has to cross between parts.
All inputs are finite; a program needn't handle non-finite values.
Results may differ from a plain program's by a relative error of at most 0.001.
Values may be sent and summed in bfloat16 or wider, within the bound.
A program may use at most 128 MiB of HBM per device.

v0:
```python
import functools

import jax
import jax.numpy as jnp
from jax import lax
from jax.experimental import pallas as pl
from jax.experimental.pallas import tpu as pltpu
from jax.sharding import PartitionSpec as P

learn_rate = 0.02
decay_rate = 0.05
tiny_value = 1e-08

LAG = 1
MESH = pl.DeviceIdType.MESH


def chunks_of(widths):
    out = []
    for a, width in enumerate(widths):
        step = 128 if width % 128 == 0 else width
        out += [(a, c, step) for c in range(0, width, step)]
    return out


def kernel(n, wide, chunks, *refs):
    inputs, norms = [refs[0:3], refs[3:6], refs[6:9]], refs[9:11]
    finals, columns, serve, results = refs[11:14], refs[14:17], refs[17], refs[18:21]
    held = [refs[21:24], refs[24:27], refs[27:30]]
    gain, sums, in_sem, gain_sem, sum_send, sum_recv, send, recv, norm_send, norm_recv = refs[30:]
    me, col = lax.axis_index("rows"), lax.axis_index("width")
    flat, group = me * wide + col, n * wide
    depth = results[0].shape[0]
    block = min(depth, 64)

    barrier = pltpu.get_barrier_semaphore()

    def greet(p, carry):
        peer = lax.rem(flat + p, group)
        pl.semaphore_signal(
            barrier, inc=1,
            device_id={"rows": lax.div(peer, wide), "width": lax.rem(peer, wide)},
            device_id_type=MESH,
        )
        return carry

    def load(j, k):
        a, c, cw = chunks[j]
        return pltpu.make_async_copy(
            inputs[a][k].at[:, pl.ds(c, cw)], held[a][k].at[:, pl.ds(c, cw)], in_sem.at[j, k]
        )

    ahead = min(2, len(chunks))
    for j in range(ahead):
        for k in range(3):
            load(j, k).start()
    for k in range(2):
        pltpu.make_async_copy(norms[k], gain.at[k], gain_sem.at[k]).start()
    lax.fori_loop(1, group, greet, 0)

    def update(j):
        a, c, cw = chunks[j]
        for k in range(3):
            load(j, k).wait()
        if j + ahead < len(chunks):
            for k in range(3):
                load(j + ahead, k).start()
        weight, moment, square = held[a]
        cols = pl.ds(c, cw)

        def body(i, acc):
            rows = pl.ds(pl.multiple_of(i * block, block), block)
            w = weight[rows, cols]
            r = w - learn_rate * (
                moment[rows, cols] / (jnp.sqrt(square[rows, cols]) + tiny_value) + decay_rate * w
            )
            results[a][rows, cols] = r
            return acc + jnp.sum((r * r).reshape(block // 8, 8, cw), axis=0)

        acc = lax.fori_loop(0, depth // block, body, jnp.zeros((8, cw), jnp.float32))
        sums[j, me, :, pl.ds(0, cw)] = jnp.sum(acc, axis=0, keepdims=True)

    def sum_copy(j, p, slot):
        return pltpu.make_async_remote_copy(
            src_ref=sums.at[j, me], dst_ref=sums.at[j, slot],
            send_sem=sum_send.at[j, p], recv_sem=sum_recv.at[j, p],
            device_id={"rows": lax.rem(me + p, n)}, device_id_type=MESH,
        )

    def norm_copy(p, slot):
        peer = lax.rem(flat + p, group)
        return pltpu.make_async_remote_copy(
            src_ref=serve.at[flat], dst_ref=serve.at[slot],
            send_sem=norm_send.at[p], recv_sem=norm_recv.at[p],
            device_id={"rows": lax.div(peer, wide), "width": lax.rem(peer, wide)},
            device_id_type=MESH,
        )

    has_next = (me < n - 1, me > 0)
    step = (1, -1)

    def pass_on(d, h, j, a, cols, origin):
        rows = pl.ds(pl.multiple_of(origin * depth, depth), depth)
        return pltpu.make_async_remote_copy(
            src_ref=finals[a].at[rows, cols], dst_ref=finals[a].at[rows, cols],
            send_sem=send.at[d, h, j], recv_sem=recv.at[d, h, j],
            device_id={"rows": lax.rem(me + step[d] + n, n)}, device_id_type=MESH,
        )

    def finish(j):
        a, c, cw = chunks[j]
        cols = pl.ds(c, cw)
        for p in range(1, n):
            sum_copy(j, p, lax.rem(me - p + n, n)).wait_recv()
        total = sums[j, 0, :, pl.ds(0, cw)]
        for p in range(1, n):
            total = total + sums[j, p, :, pl.ds(0, cw)]
        scale = jnp.sqrt(total)
        columns[a][:, cols] = scale
        inverse = 1.0 / scale

        def body(i, carry):
            rows = pl.ds(pl.multiple_of(i * block, block), block)
            mine = pl.ds(pl.multiple_of(me * depth + i * block, block), block)
            finals[a][mine, cols] = (results[a][rows, cols] * inverse).astype(jnp.bfloat16)
            return carry

        lax.fori_loop(0, depth // block, body, 0)
        for d in (0, 1):
            @pl.when(has_next[d])
            def _(d=d):
                pass_on(d, 0, j, a, cols, me).start()

    for j in range(len(chunks) + LAG):
        if j < len(chunks):
            update(j)
            if j == 0:
                pl.semaphore_wait(barrier, group - 1)
            for p in range(1, n):
                sum_copy(j, p, me).start()
        if j >= LAG:
            finish(j - LAG)

    for k in range(2):
        pltpu.make_async_copy(norms[k], gain.at[k], gain_sem.at[k]).wait()
    serve[flat] = (gain[0] + gain[1]).astype(jnp.bfloat16)

    def send_norm(p, carry):
        norm_copy(p, flat).start()
        return carry

    lax.fori_loop(1, group, send_norm, 0)

    counts = [sum(1 for ch in chunks if ch[0] == a) for a in range(3)]
    bases = [sum(counts[:a]) for a in range(3)]

    def each(visit):
        for h in range(n - 1):
            for a in range(3):
                cw = chunks[bases[a]][2]

                def body(k, carry, h=h, a=a, cw=cw):
                    start = pl.multiple_of(k * cw, 128) if counts[a] > 1 else 0
                    for d in (0, 1):
                        visit(d, h, bases[a] + k, a, pl.ds(start, cw))
                    return carry

                if counts[a] > 1:
                    lax.fori_loop(0, counts[a], body, 0)
                else:
                    body(0, 0)

    def relay(d, h, j, a, cols):
        origin = me - step[d] * (h + 1)

        @pl.when((origin >= 0) & (origin < n))
        def _():
            pass_on(d, h, j, a, cols, origin).wait_recv()

            if h + 1 < n - 1:
                @pl.when(has_next[d])
                def _():
                    pass_on(d, h + 1, j, a, cols, origin).start()

    each(relay)

    def drain(d, h, j, a, cols):
        origin = me - step[d] * h

        @pl.when(has_next[d] & (origin >= 0) & (origin < n))
        def _():
            pass_on(d, h, j, a, cols, origin).wait_send()

    each(drain)
    for j in range(len(chunks)):
        for p in range(1, n):
            sum_copy(j, p, me).wait_send()

    def end_norm(p, carry):
        norm_copy(p, lax.rem(flat - p + group, group)).wait_recv()
        norm_copy(p, flat).wait_send()
        return carry

    lax.fori_loop(1, group, end_norm, 0)


def store(pieces, *refs):
    count = len(pieces)
    sem = refs[2 * count]
    copies = []
    for k, cut in enumerate(pieces):
        rows = refs[k].shape[0] // cut
        for i in range(cut):
            part = pl.ds(i * rows, rows)
            copies.append(
                pltpu.make_async_copy(
                    refs[k].at[part], refs[count + k].at[part], sem.at[len(copies)]
                )
            )
    for copy in copies:
        copy.start()
    for copy in copies:
        copy.wait()


def solution(mesh):
    n, wide = mesh.shape["rows"], mesh.shape["width"]

    def per_device(*args):
        arrays, (norm_train, norm_step) = args[:9], args[9:]
        depth = arrays[0].shape[0]
        widths = [arrays[3 * a].shape[1] for a in range(3)]
        chunks = chunks_of(widths)
        count = len(chunks)
        part = norm_train.shape[0]
        lanes = 128 if part % 128 == 0 else part
        norms = [x.reshape(part // lanes, lanes) for x in (norm_train, norm_step)]
        group = n * wide
        vmem, dma = pltpu.VMEM, pltpu.SemaphoreType.DMA
        out_shape = (
            [vmem((n * depth, w), jnp.bfloat16) for w in widths]
            + [vmem((1, w), jnp.float32) for w in widths]
            + [vmem((group, part // lanes, lanes), jnp.bfloat16)]
            + [vmem((depth, w), jnp.float32) for w in widths]
        )
        padded = sum(-(-w // 128) * 128 for w in widths)
        outside = padded * depth * (2 * n + 4) + (1 << 20)
        outs = pl.pallas_call(
            functools.partial(kernel, n, wide, chunks),
            out_shape=out_shape,
            in_specs=[pl.BlockSpec(memory_space=pltpu.HBM)] * 11,
            out_specs=[pl.BlockSpec(memory_space=vmem)] * 10,
            scratch_shapes=[vmem((depth, w), jnp.float32) for w in widths for _ in range(3)]
            + [
                vmem((2, part // lanes, lanes), jnp.float32),
                vmem((count, n, 1, 128), jnp.float32),
                dma((count, 3)),
                dma((2,)),
                dma((count, n)),
                dma((count, n)),
                dma((2, n - 1, count)),
                dma((2, n - 1, count)),
                dma((group,)),
                dma((group,)),
            ],
            compiler_params=pltpu.CompilerParams(
                collective_id=0,
                has_side_effects=True,
                vmem_limit_bytes=60 * (1 << 20) - outside,
            ),
        )(*arrays, *norms)
        pieces = [n, 1, 1, 1, 1, 1, 1, 2, 1, 1]
        outs = pl.pallas_call(
            functools.partial(store, pieces),
            out_shape=[jax.ShapeDtypeStruct(x.shape, x.dtype) for x in outs],
            in_specs=[pl.BlockSpec(memory_space=vmem)] * 10,
            out_specs=[pl.BlockSpec(memory_space=pltpu.HBM)] * 10,
            scratch_shapes=[dma((sum(pieces),))],
            compiler_params=pltpu.CompilerParams(vmem_limit_bytes=1 << 20),
        )(*(pltpu.with_memory_space_constraint(x, vmem) for x in outs))
        return (
            *outs[0:3],
            *(c.reshape(-1) for c in outs[3:6]),
            outs[6].reshape(-1),
            *outs[7:10],
        )

    cut = P(("site", "rows"), "width")
    return jax.shard_map(
        per_device,
        mesh=mesh,
        in_specs=(cut,) * 9 + (P(("site", "rows", "width")),) * 2,
        out_specs=(P("site", "width"),) * 3
        + (P(("site", "width")),) * 3
        + (P("site"),)
        + (cut,) * 3,
        check_vma=False,
    )
```

profile of v0, /device:TPU:1, one launch (start us, length us, event | category | flops | bytes accessed | tf_op | source)
XLA Modules:
  0.0 221.0 jit_solution(6845767069021213522)
XLA Ops:
  0.6 213.7 %shard_map.186 = (bf16[4096,1024]{1,0:T(8,128)(2,1)S(1)}, bf16[4096,256]{1,0:T(8,128)(2,1)S(1)}, bf16[4096,256]{1,0:T(8,128)(2,1)S(1)}, f32[1,1024]{1,0:T(1,128)...) custom-call(f32[1024,1024]{1,0:T(8,128)} %refs_0_.1, ...), custom_call_target="tpu_custom_call" | custom-call | tf_op jit(solution)/shard_map/pallas_call | solution.py:248
  214.4 6.6 %shard_map.187 = (bf16[4096,1024]{1,0:T(8,128)(2,1)}, bf16[4096,256]{1,0:T(8,128)(2,1)}, bf16[4096,256]{1,0:T(8,128)(2,1)}, f32[1,1024]{1,0:T(1,128)}, f32[1,256...) custom-call(bf16[4096,1024]{1,0:T(8,128)(2,1)S(1)} %get-tuple-elemen, ...), custom_call_target="tpu_custom_call" | custom-call | tf_op jit(solution)/shard_map/pallas_call | solution.py:273
where the time goes:
time: 224 us; the launch traced here: 221 us
  Pallas kernels  220 us (98%)
    pallas_call x1, Pallas kernels, per_device(): pl.pallas_call(functools.partial(kernel, n, wide, chunks), out_shape=out_...  214 us
    pallas_call x1, Pallas kernels, per_device(): pl.pallas_call(functools.partial(store, pieces), out_shape=[jax.ShapeDtyp...  6.6 us

commit v1 on v0

v1 whole, which is shorter than its diff:
```python
import functools

import jax
import jax.numpy as jnp
from jax import lax
from jax.experimental import pallas as pl
from jax.experimental.pallas import tpu as pltpu
from jax.sharding import PartitionSpec as P

learn_rate = 0.02
decay_rate = 0.05
tiny_value = 1e-08

LAG = 1
HELD = 4, 8
MESH = pl.DeviceIdType.MESH


def chunks_of(widths):
    out = []
    for a, width in enumerate(widths):
        step = 128 if width % 128 == 0 else width
        out += [(a, c, step) for c in range(0, width, step)]
    return out


def late_of(chunks):
    count = sum(1 for ch in chunks if ch[0] == 0)
    return count - max(1, count * HELD[0] // HELD[1])


def waits(n, site):
    me = lax.axis_index("rows")
    late = lax.axis_index("site") == site - 1
    return me, late & (me == 0), late & (me == n - 1)


def gather(n, site, chunks, *refs):
    inputs, norms = [refs[0:3], refs[3:6], refs[6:9]], refs[9:11]
    finals, columns, gains, results = refs[11:14], refs[14:17], refs[17], refs[18:21]
    held = [refs[21:24], refs[24:27], refs[27:30]]
    gain, sums, in_sem, gain_sem, sum_send, sum_recv, send, recv, norm_send, norm_recv = refs[30:]
    me, first, last = waits(n, site)
    late = lax.axis_index("site") == site - 1
    depth = results[0].shape[0]
    block = min(depth, 64)
    split = late_of(chunks)
    counts = [sum(1 for ch in chunks if ch[0] == a) for a in range(3)]
    bases = [sum(counts[:a]) for a in range(3)]

    barrier = pltpu.get_barrier_semaphore()

    def load(j, k):
        a, c, cw = chunks[j]
        return pltpu.make_async_copy(
            inputs[a][k].at[:, pl.ds(c, cw)], held[a][k].at[:, pl.ds(c, cw)], in_sem.at[j, k]
        )

    for p in range(1, n):
        pl.semaphore_signal(
            barrier, inc=1, device_id={"rows": lax.rem(me + p, n)}, device_id_type=MESH
        )
    ahead = min(2, len(chunks))
    for j in range(ahead):
        for k in range(3):
            load(j, k).start()
    for k in range(2):
        pltpu.make_async_copy(norms[k], gain.at[k], gain_sem.at[k]).start()

    def update(j):
        a, c, cw = chunks[j]
        for k in range(3):
            load(j, k).wait()
        if j + ahead < len(chunks):
            for k in range(3):
                load(j + ahead, k).start()
        weight, moment, square = held[a]
        cols = pl.ds(c, cw)

        def body(i, acc):
            rows = pl.ds(pl.multiple_of(i * block, block), block)
            w = weight[rows, cols]
            r = w - learn_rate * (
                moment[rows, cols] / (jnp.sqrt(square[rows, cols]) + tiny_value) + decay_rate * w
            )
            results[a][rows, cols] = r
            return acc + jnp.sum((r * r).reshape(block // 8, 8, cw), axis=0)

        acc = lax.fori_loop(0, depth // block, body, jnp.zeros((8, cw), jnp.float32))
        sums[j, me, :, pl.ds(0, cw)] = jnp.sum(acc, axis=0, keepdims=True)

    def sum_copy(j, p, slot):
        return pltpu.make_async_remote_copy(
            src_ref=sums.at[j, me], dst_ref=sums.at[j, slot],
            send_sem=sum_send.at[j, p], recv_sem=sum_recv.at[j, p],
            device_id={"rows": lax.rem(me + p, n)}, device_id_type=MESH,
        )

    def norm_copy(p, slot):
        return pltpu.make_async_remote_copy(
            src_ref=gains.at[me], dst_ref=gains.at[slot],
            send_sem=norm_send.at[p], recv_sem=norm_recv.at[p],
            device_id={"rows": lax.rem(me + p, n)}, device_id_type=MESH,
        )

    has_next = (me < n - 1, me > 0)
    step = (1, -1)
    keeps = (late & (me == n - 2), late & (me == 1))
    lacks = (last, first)

    def pass_on(d, h, j, a, cols, origin):
        rows = pl.ds(pl.multiple_of(origin * depth, depth), depth)
        return pltpu.make_async_remote_copy(
            src_ref=finals[a].at[rows, cols], dst_ref=finals[a].at[rows, cols],
            send_sem=send.at[d, h, j], recv_sem=recv.at[d, h, j],
            device_id={"rows": lax.rem(me + step[d] + n, n)}, device_id_type=MESH,
        )

    def finish(j):
        a, c, cw = chunks[j]
        cols = pl.ds(c, cw)
        for p in range(1, n):
            sum_copy(j, p, lax.rem(me - p + n, n)).wait_recv()
        total = sums[j, 0, :, pl.ds(0, cw)]
        for p in range(1, n):
            total = total + sums[j, p, :, pl.ds(0, cw)]
        scale = jnp.sqrt(total)
        columns[a][:, cols] = scale
        inverse = 1.0 / scale

        def body(i, carry):
            rows = pl.ds(pl.multiple_of(i * block, block), block)
            mine = pl.ds(pl.multiple_of(me * depth + i * block, block), block)
            finals[a][mine, cols] = (results[a][rows, cols] * inverse).astype(jnp.bfloat16)
            return carry

        lax.fori_loop(0, depth // block, body, 0)
        for d in (0, 1):
            goes = has_next[d]
            if a == 0 and j >= split:
                goes = goes & jnp.logical_not(keeps[d])

            @pl.when(goes)
            def _(d=d):
                pass_on(d, 0, j, a, cols, me).start()

    for j in range(len(chunks) + LAG):
        if j < len(chunks):
            update(j)
            if j == 0:
                pl.semaphore_wait(barrier, n - 1)
            for p in range(1, n):
                sum_copy(j, p, me).start()
        if j >= LAG:
            finish(j - LAG)

    for k in range(2):
        pltpu.make_async_copy(norms[k], gain.at[k], gain_sem.at[k]).wait()
    gains[me] = (gain[0] + gain[1]).astype(jnp.bfloat16)
    for p in range(1, n):
        norm_copy(p, me).start()

    def span(a, cut, visit):
        cw = chunks[bases[a]][2]

        def body(k, carry):
            start = pl.multiple_of(k * cw, 128) if counts[a] > 1 else 0
            visit(bases[a] + k, a, pl.ds(start, cw))
            return carry

        low, high = cut
        if counts[a] > 1:
            lax.fori_loop(low, high, body, 0)
        elif high > low:
            body(0, 0)

    def parts(a, h):
        if a == 0 and h == 0:
            return ((0, split), False), ((split, counts[0]), True)
        return (((0, counts[a]), False),)

    def relay(h):
        for a in range(3):
            for cut, tail in parts(a, h):

                def visit(j, a, cols, tail=tail):
                    for d in (0, 1):
                        origin = me - step[d] * (h + 1)
                        comes = (origin >= 0) & (origin < n)
                        if tail:
                            comes = comes & jnp.logical_not(lacks[d])

                        @pl.when(comes)
                        def _(d=d, origin=origin):
                            pass_on(d, h, j, a, cols, origin).wait_recv()

                            if h + 1 < n - 1:
                                @pl.when(has_next[d])
                                def _():
                                    pass_on(d, h + 1, j, a, cols, origin).start()

                span(a, cut, visit)

    def drain(h):
        for d in (0, 1):
            origin = me - step[d] * h
            for a in range(3):
                for cut, tail in parts(a, h):
                    went = has_next[d] & (origin >= 0) & (origin < n)
                    if tail:
                        went = went & jnp.logical_not(keeps[d])

                    @pl.when(went)
                    def _(d=d, a=a, cut=cut, origin=origin):
                        span(
                            a, cut,
                            lambda j, a, cols: pass_on(d, h, j, a, cols, origin).wait_send(),
                        )

    for h in range(n - 1):
        if h == n - 2:
            for j in range(len(chunks)):
                for p in range(1, n):
                    sum_copy(j, p, me).wait_send()
            for p in range(1, n):
                norm_copy(p, lax.rem(me - p + n, n)).wait_recv()
                norm_copy(p, me).wait_send()
        relay(h)
        if h >= 1:
            drain(h - 1)
    drain(n - 2)


def store(n, site, kept, *refs):
    count = 9
    sources, gains = refs[:count], refs[count]
    targets, handed, sem = refs[count + 1 : 2 * count + 1], refs[2 * count + 1], refs[-1]
    me, first, last = waits(n, site)
    depth, width = sources[0].shape[0] // n, sources[0].shape[1]
    copies = []
    for k in range(1, count):
        copies.append(pltpu.make_async_copy(sources[k], targets[k], sem.at[len(copies)]))
    maybe = []
    for o in range(n):
        rows = pl.ds(o * depth, depth)
        if kept < width:
            part = (rows, pl.ds(0, width - kept))
            copies.append(
                pltpu.make_async_copy(
                    sources[0].at[part], targets[0].at[part], sem.at[len(copies)]
                )
            )
        lacks = jnp.bool_(False)
        if o == 1:
            lacks = lacks | first
        if o == n - 2:
            lacks = lacks | last
        part = (rows, pl.ds(width - kept, kept))
        maybe.append(
            (
                jnp.logical_not(lacks),
                pltpu.make_async_copy(
                    sources[0].at[part], targets[0].at[part], sem.at[count - 1 + n + o]
                ),
            )
        )
    for copy in copies:
        copy.start()
    for has, copy in maybe:
        pl.when(has)(copy.start)
    handed[...] = gains[...]
    for copy in copies:
        copy.wait()
    for has, copy in maybe:
        pl.when(has)(copy.wait)


def finish_gather(n, wide, site, final, gains, piece, serve, send, recv, norm_send, norm_recv):
    me, first, last = waits(n, site)
    late = lax.axis_index("site") == site - 1
    col = lax.axis_index("width")
    depth, kept = piece.shape
    width = final.shape[1]
    keeps = (late & (me == n - 2), late & (me == 1))
    lacks = (last, first)
    step = (1, -1)

    barrier = pltpu.get_barrier_semaphore()
    for p in range(1, wide):
        pl.semaphore_signal(
            barrier, inc=1, device_id={"width": lax.rem(col + p, wide)}, device_id_type=MESH
        )
    for d in (0, 1):
        for has, way in ((keeps[d], step[d]), (lacks[d], -step[d])):
            @pl.when(has)
            def _(way=way):
                pl.semaphore_signal(
                    barrier, inc=1, device_id={"rows": lax.rem(me + way + n, n)},
                    device_id_type=MESH,
                )
    extra = sum(x.astype(jnp.int32) for x in (*keeps, *lacks))
    pl.semaphore_wait(barrier, wide - 1 + extra)

    def tail(d):
        rows = pl.ds(pl.multiple_of(me * depth, depth), depth)
        return pltpu.make_async_remote_copy(
            src_ref=final.at[rows, pl.ds(width - kept, kept)], dst_ref=piece,
            send_sem=send.at[d], recv_sem=recv.at[d],
            device_id={"rows": lax.rem(me + step[d] + n, n)}, device_id_type=MESH,
        )

    def norm_copy(p, slot):
        return pltpu.make_async_remote_copy(
            src_ref=gains, dst_ref=serve.at[:, slot],
            send_sem=norm_send.at[p], recv_sem=norm_recv.at[p],
            device_id={"width": lax.rem(col + p, wide)}, device_id_type=MESH,
        )

    for d in (0, 1):
        pl.when(keeps[d])(tail(d).start)
    for p in range(1, wide):
        norm_copy(p, col).start()
    serve[:, col] = gains[...]
    for p in range(1, wide):
        norm_copy(p, lax.rem(col - p + wide, wide)).wait_recv()
        norm_copy(p, col).wait_send()
    for d in (0, 1):
        pl.when(keeps[d])(tail(d).wait_send)
        pl.when(lacks[d])(tail(d).wait_recv)


def finish_store(n, site, query, piece, serve, out, served, sem):
    me, first, last = waits(n, site)
    depth, kept = piece.shape
    width = out.shape[1]
    copies = [(None, pltpu.make_async_copy(serve, served, sem.at[0]))]
    for has, origin in ((first, 1), (last, n - 2)):
        part = (pl.ds(origin * depth, depth), pl.ds(width - kept, kept))
        copies.append((has, pltpu.make_async_copy(piece, out.at[part], sem.at[len(copies)])))
    for has, copy in copies:
        copy.start() if has is None else pl.when(has)(copy.start)
    for has, copy in copies:
        copy.wait() if has is None else pl.when(has)(copy.wait)


def solution(mesh):
    n, wide, site = mesh.shape["rows"], mesh.shape["width"], mesh.shape["site"]

    def per_device(*args):
        arrays, (norm_train, norm_step) = args[:9], args[9:]
        depth = arrays[0].shape[0]
        widths = [arrays[3 * a].shape[1] for a in range(3)]
        chunks = chunks_of(widths)
        count = len(chunks)
        kept = widths[0] - chunks[late_of(chunks)][1]
        part = norm_train.shape[0]
        lanes = 128 if part % 128 == 0 else part
        norms = [x.reshape(part // lanes, lanes) for x in (norm_train, norm_step)]
        vmem, dma, hbm = pltpu.VMEM, pltpu.SemaphoreType.DMA, pltpu.HBM
        in_vmem, in_hbm = pl.BlockSpec(memory_space=vmem), pl.BlockSpec(memory_space=hbm)

        def pinned(x):
            return pltpu.with_memory_space_constraint(x, vmem)

        def shaped(x):
            return jax.ShapeDtypeStruct(x.shape, x.dtype)

        out_shape = (
            [vmem((n * depth, w), jnp.bfloat16) for w in widths]
            + [vmem((1, w), jnp.float32) for w in widths]
            + [vmem((n, part // lanes, lanes), jnp.bfloat16)]
            + [vmem((depth, w), jnp.float32) for w in widths]
        )
        padded = sum(-(-w // 128) * 128 for w in widths)
        outside = padded * depth * (2 * n + 4) + (1 << 20)
        outs = pl.pallas_call(
            functools.partial(gather, n, site, chunks),
            out_shape=out_shape,
            in_specs=[in_hbm] * 11,
            out_specs=[in_vmem] * 10,
            scratch_shapes=[vmem((depth, w), jnp.float32) for w in widths for _ in range(3)]
            + [
                vmem((2, part // lanes, lanes), jnp.float32),
                vmem((count, n, 1, 128), jnp.float32),
                dma((count, 3)),
                dma((2,)),
                dma((count, n)),
                dma((count, n)),
                dma((2, n - 1, count)),
                dma((2, n - 1, count)),
                dma((n,)),
                dma((n,)),
            ],
            compiler_params=pltpu.CompilerParams(
                collective_id=0,
                has_side_effects=True,
                vmem_limit_bytes=60 * (1 << 20) - outside,
            ),
        )(*arrays, *norms)
        outs = [pinned(x) for x in outs]
        first = outs[0:6] + outs[7:10]
        stored = pl.pallas_call(
            functools.partial(store, n, site, kept),
            out_shape=[shaped(x) for x in first] + [out_shape[6]],
            in_specs=[in_vmem] * 10,
            out_specs=[in_hbm] * 9 + [in_vmem],
            scratch_shapes=[dma((8 + 2 * n,))],
            compiler_params=pltpu.CompilerParams(vmem_limit_bytes=1 << 20),
        )(*first, outs[6])
        piece, serve = pl.pallas_call(
            functools.partial(finish_gather, n, wide, site),
            out_shape=[
                vmem((depth, kept), jnp.bfloat16),
                vmem((n, wide, part // lanes, lanes), jnp.bfloat16),
            ],
            in_specs=[in_vmem] * 2,
            out_specs=[in_vmem] * 2,
            scratch_shapes=[dma((2,)), dma((2,)), dma((wide,)), dma((wide,))],
            compiler_params=pltpu.CompilerParams(
                collective_id=1, has_side_effects=True, vmem_limit_bytes=1 << 20
            ),
        )(outs[0], pinned(stored[9]))
        query, serve = pl.pallas_call(
            functools.partial(finish_store, n, site),
            out_shape=[shaped(stored[0]), shaped(serve)],
            in_specs=[in_hbm, in_vmem, in_vmem],
            out_specs=[in_hbm] * 2,
            scratch_shapes=[dma((3,))],
            input_output_aliases={0: 0},
            compiler_params=pltpu.CompilerParams(vmem_limit_bytes=1 << 20),
        )(stored[0], pinned(piece), pinned(serve))
        return (
            query,
            *stored[1:3],
            *(c.reshape(-1) for c in stored[3:6]),
            serve.reshape(-1),
            *stored[6:9],
        )

    cut = P(("site", "rows"), "width")
    return jax.shard_map(
        per_device,
        mesh=mesh,
        in_specs=(cut,) * 9 + (P(("site", "rows", "width")),) * 2,
        out_specs=(P("site", "width"),) * 3
        + (P(("site", "width")),) * 3
        + (P("site"),)
        + (cut,) * 3,
        check_vma=False,
    )
```

time: 224 us -> 230 us (1.027); the launches traced: 221 us -> 230 us
  Pallas kernels: 220 us -> 229 us
    pallas_call x2 -> x4, Pallas kernels: 220 us -> 229 us  [the longest x1 208 us: per_device(): pl.pallas_call(functools.partial(gather, n, site, chunks), out_shape=out_...]
where the time goes in v1:
time: 230 us
  Pallas kernels  229 us (100%)
    pallas_call x1, Pallas kernels, per_device(): pl.pallas_call(functools.partial(gather, n, site, chunks), out_shape=out_...  208 us
    pallas_call x1, Pallas kernels, per_device(): pl.pallas_call(functools.partial(finish_gather, n, wide, site), out_shape...  14.1 us
    pallas_call x1, Pallas kernels, per_device(): pl.pallas_call(functools.partial(store, n, site, kept), out_shape=[shaped...  6.3 us

profile of v1, /device:TPU:1, one launch (start us, length us, event | category | flops | bytes accessed | tf_op | source)
XLA Modules:
  0.0 230.0 jit_solution(2074216143357816766)
XLA Ops:
  0.6 207.9 %shard_map.186 = (bf16[4096,1024]{1,0:T(8,128)(2,1)S(1)}, bf16[4096,256]{1,0:T(8,128)(2,1)S(1)}, bf16[4096,256]{1,0:T(8,128)(2,1)S(1)}, f32[1,1024]{1,0:T(1,128)...) custom-call(f32[1024,1024]{1,0:T(8,128)} %refs_0_.1, ...), custom_call_target="tpu_custom_call" | custom-call | tf_op jit(solution)/shard_map/pallas_call | solution.py:376
  208.6 6.3 %shard_map.187 = (bf16[4096,1024]{1,0:T(8,128)(2,1)}, bf16[4096,256]{1,0:T(8,128)(2,1)}, bf16[4096,256]{1,0:T(8,128)(2,1)}, f32[1,1024]{1,0:T(1,128)}, f32[1,256...) custom-call(bf16[4096,1024]{1,0:T(8,128)(2,1)S(1)} %get-tuple-elemen, ...), custom_call_target="tpu_custom_call" | custom-call | tf_op jit(solution)/shard_map/pallas_call | solution.py:402
  214.9 14.1 %shard_map.188 = (bf16[1024,512]{1,0:T(8,128)(2,1)S(1)}, bf16[4,4,2,128]{3,2,1,0:T(2,128)(2,1)S(1)}) custom-call(bf16[4096,1024]{1,0:T(8,128)(2,1)S(1)} %get-tuple-element.34.refs_0_.final, bf16[4,2,128]{2,1,0:T(2,128)(2,1)S(1)} %get-tuple-element.45.gains), custom_call_target="tpu_custom_call" | custom-call | tf_op jit(solution)/shard_map/pallas_call | solution.py:410
  228.9 1.0 shard_map.189

commit v2 on v1

--- a/solution.py
+++ b/solution.py
@@ -11,7 +11,8 @@
 decay_rate = 0.05
 tiny_value = 1e-08
 
-LAG = 1
+LEAD = 4
+AHEAD = 4
 HELD = 4, 8
 MESH = pl.DeviceIdType.MESH
 
@@ -35,13 +36,15 @@
     return me, late & (me == 0), late & (me == n - 1)
 
 
-def gather(n, site, chunks, *refs):
+def gather(n, wide, site, chunks, *refs):
     inputs, norms = [refs[0:3], refs[3:6], refs[6:9]], refs[9:11]
-    finals, columns, gains, results = refs[11:14], refs[14:17], refs[17], refs[18:21]
+    finals, columns, serve, results = refs[11:14], refs[14:17], refs[17], refs[18:21]
     held = [refs[21:24], refs[24:27], refs[27:30]]
-    gain, sums, in_sem, gain_sem, sum_send, sum_recv, send, recv, norm_send, norm_recv = refs[30:]
+    gain, sums, in_sem, gain_sem, sum_send, sum_recv, send, recv = refs[30:38]
+    norm_send, norm_recv, wide_send, wide_recv = refs[38:]
     me, first, last = waits(n, site)
     late = lax.axis_index("site") == site - 1
+    col = lax.axis_index("width")
     depth = results[0].shape[0]
     block = min(depth, 64)
     split = late_of(chunks)
@@ -60,7 +63,11 @@
         pl.semaphore_signal(
             barrier, inc=1, device_id={"rows": lax.rem(me + p, n)}, device_id_type=MESH
         )
-    ahead = min(2, len(chunks))
+    for p in range(1, wide):
+        pl.semaphore_signal(
+            barrier, inc=1, device_id={"width": lax.rem(col + p, wide)}, device_id_type=MESH
+        )
+    ahead = min(AHEAD, len(chunks))
     for j in range(ahead):
         for k in range(3):
             load(j, k).start()
@@ -98,9 +105,16 @@
 
     def norm_copy(p, slot):
         return pltpu.make_async_remote_copy(
-            src_ref=gains.at[me], dst_ref=gains.at[slot],
+            src_ref=serve.at[me, col], dst_ref=serve.at[slot, col],
             send_sem=norm_send.at[p], recv_sem=norm_recv.at[p],
             device_id={"rows": lax.rem(me + p, n)}, device_id_type=MESH,
+        )
+
+    def wide_copy(p, slot):
+        return pltpu.make_async_remote_copy(
+            src_ref=serve.at[:, col], dst_ref=serve.at[:, slot],
+            send_sem=wide_send.at[p], recv_sem=wide_recv.at[p],
+            device_id={"width": lax.rem(col + p, wide)}, device_id_type=MESH,
         )
 
     has_next = (me < n - 1, me > 0)
@@ -144,19 +158,20 @@
             def _(d=d):
                 pass_on(d, 0, j, a, cols, me).start()
 
-    for j in range(len(chunks) + LAG):
-        if j < len(chunks):
-            update(j)
-            if j == 0:
-                pl.semaphore_wait(barrier, n - 1)
+    ready = 0
+    for j in range(len(chunks)):
+        while ready < min(len(chunks), LEAD * (j + 1)):
+            update(ready)
+            if ready == 0:
+                pl.semaphore_wait(barrier, n + wide - 2)
             for p in range(1, n):
-                sum_copy(j, p, me).start()
-        if j >= LAG:
-            finish(j - LAG)
+                sum_copy(ready, p, me).start()
+            ready += 1
+        finish(j)
 
     for k in range(2):
         pltpu.make_async_copy(norms[k], gain.at[k], gain_sem.at[k]).wait()
-    gains[me] = (gain[0] + gain[1]).astype(jnp.bfloat16)
+    serve[me, col] = (gain[0] + gain[1]).astype(jnp.bfloat16)
     for p in range(1, n):
         norm_copy(p, me).start()
 
@@ -223,18 +238,25 @@
                 for p in range(1, n):
                     sum_copy(j, p, me).wait_send()
             for p in range(1, n):
+                norm_copy(p, me).wait_send()
+            for p in range(1, wide):
+                wide_copy(p, col).wait_send()
+                wide_copy(p, lax.rem(col - p + wide, wide)).wait_recv()
+        relay(h)
+        if h == 0:
+            for p in range(1, n):
                 norm_copy(p, lax.rem(me - p + n, n)).wait_recv()
-                norm_copy(p, me).wait_send()
-        relay(h)
+            for p in range(1, wide):
+                wide_copy(p, col).start()
         if h >= 1:
             drain(h - 1)
     drain(n - 2)
 
 
 def store(n, site, kept, *refs):
-    count = 9
-    sources, gains = refs[:count], refs[count]
-    targets, handed, sem = refs[count + 1 : 2 * count + 1], refs[2 * count + 1], refs[-1]
+    count = 10
+    sources, targets = refs[:count], refs[count : 2 * count]
+    handed, sem = refs[2 * count :]
     me, first, last = waits(n, site)
     depth, width = sources[0].shape[0] // n, sources[0].shape[1]
     copies = []
@@ -268,17 +290,16 @@
         copy.start()
     for has, copy in maybe:
         pl.when(has)(copy.start)
-    handed[...] = gains[...]
+    handed[...] = sources[3][...]
     for copy in copies:
         copy.wait()
     for has, copy in maybe:
         pl.when(has)(copy.wait)
 
 
-def finish_gather(n, wide, site, final, gains, piece, serve, send, recv, norm_send, norm_recv):
+def finish_gather(n, site, final, after, piece, send, recv):
     me, first, last = waits(n, site)
     late = lax.axis_index("site") == site - 1
-    col = lax.axis_index("width")
     depth, kept = piece.shape
     width = final.shape[1]
     keeps = (late & (me == n - 2), late & (me == 1))
@@ -286,20 +307,21 @@
     step = (1, -1)
 
     barrier = pltpu.get_barrier_semaphore()
-    for p in range(1, wide):
-        pl.semaphore_signal(
-            barrier, inc=1, device_id={"width": lax.rem(col + p, wide)}, device_id_type=MESH
-        )
+    count = jnp.int32(0)
     for d in (0, 1):
         for has, way in ((keeps[d], step[d]), (lacks[d], -step[d])):
+            count = count + has.astype(jnp.int32)
+
             @pl.when(has)
             def _(way=way):
                 pl.semaphore_signal(
                     barrier, inc=1, device_id={"rows": lax.rem(me + way + n, n)},
                     device_id_type=MESH,
                 )
-    extra = sum(x.astype(jnp.int32) for x in (*keeps, *lacks))
-    pl.semaphore_wait(barrier, wide - 1 + extra)
+
+    @pl.when(count > 0)
+    def _():
+        pl.semaphore_wait(barrier, count)
 
     def tail(d):
         rows = pl.ds(pl.multiple_of(me * depth, depth), depth)
@@ -309,38 +331,25 @@
             device_id={"rows": lax.rem(me + step[d] + n, n)}, device_id_type=MESH,
         )
 
-    def norm_copy(p, slot):
-        return pltpu.make_async_remote_copy(
-            src_ref=gains, dst_ref=serve.at[:, slot],
-            send_sem=norm_send.at[p], recv_sem=norm_recv.at[p],
-            device_id={"width": lax.rem(col + p, wide)}, device_id_type=MESH,
-        )
-
     for d in (0, 1):
         pl.when(keeps[d])(tail(d).start)
-    for p in range(1, wide):
-        norm_copy(p, col).start()
-    serve[:, col] = gains[...]
-    for p in range(1, wide):
-        norm_copy(p, lax.rem(col - p + wide, wide)).wait_recv()
-        norm_copy(p, col).wait_send()
     for d in (0, 1):
         pl.when(keeps[d])(tail(d).wait_send)
         pl.when(lacks[d])(tail(d).wait_recv)
 
 
-def finish_store(n, site, query, piece, serve, out, served, sem):
+def finish_store(n, site, query, piece, out, sem):
     me, first, last = waits(n, site)
     depth, kept = piece.shape
     width = out.shape[1]
-    copies = [(None, pltpu.make_async_copy(serve, served, sem.at[0]))]
     for has, origin in ((first, 1), (last, n - 2)):
         part = (pl.ds(origin * depth, depth), pl.ds(width - kept, kept))
-        copies.append((has, pltpu.make_async_copy(piece, out.at[part], sem.at[len(copies)])))
-    for has, copy in copies:
-        copy.start() if has is None else pl.when(has)(copy.start)
-    for has, copy in copies:
-        copy.wait() if has is None else pl.when(has)(copy.wait)
+
+        @pl.when(has)
+        def _(part=part):
+            copy = pltpu.make_async_copy(piece, out.at[part], sem)
+            copy.start()
+            copy.wait()
 
 
 def solution(mesh):
@@ -368,13 +377,13 @@
         out_shape = (
             [vmem((n * depth, w), jnp.bfloat16) for w in widths]
             + [vmem((1, w), jnp.float32) for w in widths]
-            + [vmem((n, part // lanes, lanes), jnp.bfloat16)]
+            + [vmem((n, wide, part // lanes, lanes), jnp.bfloat16)]
             + [vmem((depth, w), jnp.float32) for w in widths]
         )
         padded = sum(-(-w // 128) * 128 for w in widths)
         outside = padded * depth * (2 * n + 4) + (1 << 20)
         outs = pl.pallas_call(
-            functools.partial(gather, n, site, chunks),
+            functools.partial(gather, n, wide, site, chunks),
             out_shape=out_shape,
             in_specs=[in_hbm] * 11,
             out_specs=[in_vmem] * 10,
@@ -390,6 +399,8 @@
                 dma((2, n - 1, count)),
                 dma((n,)),
                 dma((n,)),
+                dma((wide,)),
+                dma((wide,)),
             ],
             compiler_params=pltpu.CompilerParams(
                 collective_id=0,
@@ -398,43 +409,39 @@
             ),
         )(*arrays, *norms)
         outs = [pinned(x) for x in outs]
-        first = outs[0:6] + outs[7:10]
         stored = pl.pallas_call(
             functools.partial(store, n, site, kept),
-            out_shape=[shaped(x) for x in first] + [out_shape[6]],
+            out_shape=[shaped(x) for x in outs] + [out_shape[3]],
             in_specs=[in_vmem] * 10,
-            out_specs=[in_hbm] * 9 + [in_vmem],
-            scratch_shapes=[dma((8 + 2 * n,))],
+            out_specs=[in_hbm] * 10 + [in_vmem],
+            scratch_shapes=[dma((9 + 2 * n,))],
             compiler_params=pltpu.CompilerParams(vmem_limit_bytes=1 << 20),
-        )(*first, outs[6])
-        piece, serve = pl.pallas_call(
-            functools.partial(finish_gather, n, wide, site),
-            out_shape=[
-                vmem((depth, kept), jnp.bfloat16),
-                vmem((n, wide, part // lanes, lanes), jnp.bfloat16),
-            ],
+        )(*outs)
+        piece = pl.pallas_call(
+            functools.partial(finish_gather, n, site),
+            out_shape=vmem((depth, kept), jnp.bfloat16),
             in_specs=[in_vmem] * 2,
-            out_specs=[in_vmem] * 2,
-            scratch_shapes=[dma((2,)), dma((2,)), dma((wide,)), dma((wide,))],
+            out_specs=in_vmem,
+            scratch_shapes=[dma((2,)), dma((2,))],
             compiler_params=pltpu.CompilerParams(
                 collective_id=1, has_side_effects=True, vmem_limit_bytes=1 << 20
             ),
-        )(outs[0], pinned(stored[9]))
-        query, serve = pl.pallas_call(
+        )(outs[0], pinned(stored[10]))
+        query = pl.pallas_call(
             functools.partial(finish_store, n, site),
-            out_shape=[shaped(stored[0]), shaped(serve)],
-            in_specs=[in_hbm, in_vmem, in_vmem],
-            out_specs=[in_hbm] * 2,
-            scratch_shapes=[dma((3,))],
+            out_shape=shaped(stored[0]),
+            in_specs=[in_hbm, in_vmem],
+            out_specs=in_hbm,
+            scratch_shapes=[pltpu.SemaphoreType.DMA],
             input_output_aliases={0: 0},
             compiler_params=pltpu.CompilerParams(vmem_limit_bytes=1 << 20),
-        )(stored[0], pinned(piece), pinned(serve))
+        )(stored[0], pinned(piece))
         return (
             query,
             *stored[1:3],
             *(c.reshape(-1) for c in stored[3:6]),
-            serve.reshape(-1),
-            *stored[6:9],
+            stored[6].reshape(-1),
+            *stored[7:10],
         )
 
     cut = P(("site", "rows"), "width")

time: 230 us -> 213 us (0.926)
  Pallas kernels: 229 us -> 212 us
    pallas_call x3, Pallas kernels: 223 us -> 206 us  [the longest x1 190 us: per_device(): pl.pallas_call(functools.partial(gather, n, wide, site, chunks), out_shap...]
where the time goes in v2:
time: 213 us
  Pallas kernels  212 us (100%)
    pallas_call x1, Pallas kernels, per_device(): pl.pallas_call(functools.partial(gather, n, wide, site, chunks), out_shap...  190 us
    pallas_call x1, Pallas kernels, per_device(): pl.pallas_call(functools.partial(finish_gather, n, site), out_shape=vmem(...  15.2 us
    pallas_call x1, Pallas kernels, per_device(): pl.pallas_call(functools.partial(store, n, site, kept), out_shape=[shaped...  6.31 us

profile of v2, /device:TPU:1, one launch (start us, length us, event | category | flops | bytes accessed | tf_op | source)
XLA Modules:
  0.0 213.0 jit_solution(6644866566366714008)
XLA Ops:
  0.6 189.7 %shard_map.186 = (bf16[4096,1024]{1,0:T(8,128)(2,1)S(1)}, bf16[4096,256]{1,0:T(8,128)(2,1)S(1)}, bf16[4096,256]{1,0:T(8,128)(2,1)S(1)}, f32[1,1024]{1,0:T(1,128)...) custom-call(f32[1024,1024]{1,0:T(8,128)} %refs_0_.1, ...), custom_call_target="tpu_custom_call" | custom-call | tf_op jit(solution)/shard_map/pallas_call | solution.py:385
  190.4 6.3 %shard_map.187 = (bf16[4096,1024]{1,0:T(8,128)(2,1)}, bf16[4096,256]{1,0:T(8,128)(2,1)}, bf16[4096,256]{1,0:T(8,128)(2,1)}, f32[1,1024]{1,0:T(1,128)}, f32[1,256...) custom-call(bf16[4096,1024]{1,0:T(8,128)(2,1)S(1)} %get-tuple-elemen, ...), custom_call_target="tpu_custom_call" | custom-call | tf_op jit(solution)/shard_map/pallas_call | solution.py:412
  196.7 15.2 %shard_map.188.piece = bf16[1024,512]{1,0:T(8,128)(2,1)S(1)} custom-call(bf16[4096,1024]{1,0:T(8,128)(2,1)S(1)} %get-tuple-element.31.refs_0_.final, f32[1,1024]{1,0:T(1,128)S(1)} %get-tuple-element.42.after), custom_call_target="tpu_custom_call" | custom-call | tf_op jit(solution)/shard_map/pallas_call | solution.py:420
  212.0 1.0 shard_map.189

commit v3 on v2

--- a/solution.py
+++ b/solution.py
@@ -14,6 +14,7 @@
 LEAD = 4
 AHEAD = 4
 HELD = 4, 8
+HEAD = 5, 16
 MESH = pl.DeviceIdType.MESH
 
 
@@ -30,6 +31,14 @@
     return count - max(1, count * HELD[0] // HELD[1])
 
 
+def head_of(depth, block):
+    return block * max(1, depth // block * HEAD[0] // HEAD[1])
+
+
+def block_of(depth):
+    return min(depth, 64)
+
+
 def waits(n, site):
     me = lax.axis_index("rows")
     late = lax.axis_index("site") == site - 1
@@ -41,12 +50,13 @@
     finals, columns, serve, results = refs[11:14], refs[14:17], refs[17], refs[18:21]
     held = [refs[21:24], refs[24:27], refs[27:30]]
     gain, sums, in_sem, gain_sem, sum_send, sum_recv, send, recv = refs[30:38]
-    norm_send, norm_recv, wide_send, wide_recv = refs[38:]
+    norm_send, norm_recv, wide_send, wide_recv, raw, top_sem, raw_send, raw_recv = refs[38:]
     me, first, last = waits(n, site)
     late = lax.axis_index("site") == site - 1
     col = lax.axis_index("width")
     depth = results[0].shape[0]
-    block = min(depth, 64)
+    block = block_of(depth)
+    top = head_of(depth, block)
     split = late_of(chunks)
     counts = [sum(1 for ch in chunks if ch[0] == a) for a in range(3)]
     bases = [sum(counts[:a]) for a in range(3)]
@@ -55,9 +65,14 @@
 
     def load(j, k):
         a, c, cw = chunks[j]
+        part = (pl.ds(0, depth) if j else pl.ds(top, depth - top), pl.ds(c, cw))
         return pltpu.make_async_copy(
-            inputs[a][k].at[:, pl.ds(c, cw)], held[a][k].at[:, pl.ds(c, cw)], in_sem.at[j, k]
-        )
+            inputs[a][k].at[part], held[a][k].at[part], in_sem.at[j, k]
+        )
+
+    def load_top(k):
+        part = (pl.ds(0, top), pl.ds(0, chunks[0][2]))
+        return pltpu.make_async_copy(inputs[0][k].at[part], held[0][k].at[part], top_sem.at[k])
 
     for p in range(1, n):
         pl.semaphore_signal(
@@ -68,19 +83,16 @@
             barrier, inc=1, device_id={"width": lax.rem(col + p, wide)}, device_id_type=MESH
         )
     ahead = min(AHEAD, len(chunks))
+    for k in range(3):
+        load_top(k).start()
     for j in range(ahead):
         for k in range(3):
             load(j, k).start()
     for k in range(2):
         pltpu.make_async_copy(norms[k], gain.at[k], gain_sem.at[k]).start()
 
-    def update(j):
+    def rows_of(j, low, high, acc):
         a, c, cw = chunks[j]
-        for k in range(3):
-            load(j, k).wait()
-        if j + ahead < len(chunks):
-            for k in range(3):
-                load(j + ahead, k).start()
         weight, moment, square = held[a]
         cols = pl.ds(c, cw)
 
@@ -93,7 +105,16 @@
             results[a][rows, cols] = r
             return acc + jnp.sum((r * r).reshape(block // 8, 8, cw), axis=0)
 
-        acc = lax.fori_loop(0, depth // block, body, jnp.zeros((8, cw), jnp.float32))
+        return lax.fori_loop(low // block, high // block, body, acc)
+
+    def update(j, low, acc):
+        cw = chunks[j][2]
+        for k in range(3):
+            load(j, k).wait()
+        if j + ahead < len(chunks):
+            for k in range(3):
+                load(j + ahead, k).start()
+        acc = rows_of(j, low, depth, acc)
         sums[j, me, :, pl.ds(0, cw)] = jnp.sum(acc, axis=0, keepdims=True)
 
     def sum_copy(j, p, slot):
@@ -122,8 +143,18 @@
     keeps = (late & (me == n - 2), late & (me == 1))
     lacks = (last, first)
 
-    def pass_on(d, h, j, a, cols, origin):
-        rows = pl.ds(pl.multiple_of(origin * depth, depth), depth)
+    opens = ((me == n - 2), (me == 1))
+    opened = ((me == n - 1), (me == 0))
+
+    def raw_copy(d):
+        return pltpu.make_async_remote_copy(
+            src_ref=results[0].at[pl.ds(0, top), pl.ds(0, chunks[0][2])], dst_ref=raw,
+            send_sem=raw_send.at[d], recv_sem=raw_recv.at[d],
+            device_id={"rows": lax.rem(me + step[d] + n, n)}, device_id_type=MESH,
+        )
+
+    def pass_on(d, h, j, a, cols, origin, skip=0):
+        rows = pl.ds(pl.multiple_of(origin * depth + skip, block), depth - skip)
         return pltpu.make_async_remote_copy(
             src_ref=finals[a].at[rows, cols], dst_ref=finals[a].at[rows, cols],
             send_sem=send.at[d, h, j], recv_sem=recv.at[d, h, j],
@@ -153,6 +184,9 @@
             goes = has_next[d]
             if a == 0 and j >= split:
                 goes = goes & jnp.logical_not(keeps[d])
+            if j == 0:
+                goes = goes & jnp.logical_not(opens[d])
+                pl.when(opens[d])(pass_on(d, 0, j, a, cols, me, top).start)
 
             @pl.when(goes)
             def _(d=d):
@@ -161,9 +195,16 @@
     ready = 0
     for j in range(len(chunks)):
         while ready < min(len(chunks), LEAD * (j + 1)):
-            update(ready)
+            acc, low = jnp.zeros((8, chunks[ready][2]), jnp.float32), 0
             if ready == 0:
+                low = top
+                for k in range(3):
+                    load_top(k).wait()
+                acc = rows_of(0, 0, top, acc)
                 pl.semaphore_wait(barrier, n + wide - 2)
+                for d in (0, 1):
+                    pl.when(opens[d])(raw_copy(d).start)
+            update(ready, low, acc)
             for p in range(1, n):
                 sum_copy(ready, p, me).start()
             ready += 1
@@ -175,6 +216,22 @@
     for p in range(1, n):
         norm_copy(p, me).start()
 
+    for d in (0, 1):
+        @pl.when(opened[d])
+        def _(d=d):
+            raw_copy(d).wait_recv()
+            cw = chunks[0][2]
+            inverse = 1.0 / columns[0][:, pl.ds(0, cw)]
+            origin = (n - 2, 1)[d] * depth
+
+            def body(i, carry):
+                rows = pl.ds(pl.multiple_of(i * block, block), block)
+                theirs = pl.ds(pl.multiple_of(origin + i * block, block), block)
+                finals[0][theirs, pl.ds(0, cw)] = (raw[rows, :] * inverse).astype(jnp.bfloat16)
+                return carry
+
+            lax.fori_loop(0, top // block, body, 0)
+
     def span(a, cut, visit):
         cw = chunks[bases[a]][2]
 
@@ -189,21 +246,28 @@
         elif high > low:
             body(0, 0)
 
+    whole, tail, head = range(3)
+
     def parts(a, h):
         if a == 0 and h == 0:
-            return ((0, split), False), ((split, counts[0]), True)
-        return (((0, counts[a]), False),)
+            return ((0, 1), head), ((1, split), whole), ((split, counts[0]), tail)
+        return (((0, counts[a]), whole),)
 
     def relay(h):
         for a in range(3):
-            for cut, tail in parts(a, h):
-
-                def visit(j, a, cols, tail=tail):
+            for cut, kind in parts(a, h):
+
+                def visit(j, a, cols, kind=kind):
                     for d in (0, 1):
                         origin = me - step[d] * (h + 1)
                         comes = (origin >= 0) & (origin < n)
-                        if tail:
+                        if kind == tail:
                             comes = comes & jnp.logical_not(lacks[d])
+                        if kind == head:
+                            comes = comes & jnp.logical_not(opened[d])
+                            pl.when(opened[d])(
+                                pass_on(d, h, j, a, cols, origin, top).wait_recv
+                            )
 
                         @pl.when(comes)
                         def _(d=d, origin=origin):
@@ -220,10 +284,18 @@
         for d in (0, 1):
             origin = me - step[d] * h
             for a in range(3):
-                for cut, tail in parts(a, h):
+                for cut, kind in parts(a, h):
                     went = has_next[d] & (origin >= 0) & (origin < n)
-                    if tail:
+                    if kind == tail:
                         went = went & jnp.logical_not(keeps[d])
+                    if kind == head:
+                        went = went & jnp.logical_not(opens[d])
+
+                        @pl.when(opens[d])
+                        def _(d=d):
+                            raw_copy(d).wait_send()
+                            cols = pl.ds(0, chunks[0][2])
+                            pass_on(d, 0, 0, 0, cols, me, top).wait_send()
 
                     @pl.when(went)
                     def _(d=d, a=a, cut=cut, origin=origin):
@@ -401,6 +473,10 @@
                 dma((n,)),
                 dma((wide,)),
                 dma((wide,)),
+                vmem((head_of(depth, block_of(depth)), chunks[0][2]), jnp.float32),
+                dma((3,)),
+                dma((2,)),
+                dma((2,)),
             ],
             compiler_params=pltpu.CompilerParams(
                 collective_id=0,

time: 213 us -> 212 us (level)
  no operation moved by 1% of the time
where the time goes in v3:
time: 212 us
  Pallas kernels  211 us (100%)
    pallas_call x1, Pallas kernels, per_device(): pl.pallas_call(functools.partial(gather, n, wide, site, chunks), out_shap...  189 us
    pallas_call x1, Pallas kernels, per_device(): pl.pallas_call(functools.partial(finish_gather, n, site), out_shape=vmem(...  15 us
    pallas_call x1, Pallas kernels, per_device(): pl.pallas_call(functools.partial(store, n, site, kept), out_shape=[shaped...  6.31 us

profile of v3, /device:TPU:1, one launch (start us, length us, event | category | flops | bytes accessed | tf_op | source)
XLA Modules:
  0.0 211.6 jit_solution(13800369976515276323)
XLA Ops:
  0.6 188.6 %shard_map.186 = (bf16[4096,1024]{1,0:T(8,128)(2,1)S(1)}, bf16[4096,256]{1,0:T(8,128)(2,1)S(1)}, bf16[4096,256]{1,0:T(8,128)(2,1)S(1)}, f32[1,1024]{1,0:T(1,128)...) custom-call(f32[1024,1024]{1,0:T(8,128)} %refs_0_.1, ...), custom_call_target="tpu_custom_call" | custom-call | tf_op jit(solution)/shard_map/pallas_call | solution.py:457
  189.3 6.3 %shard_map.187 = (bf16[4096,1024]{1,0:T(8,128)(2,1)}, bf16[4096,256]{1,0:T(8,128)(2,1)}, bf16[4096,256]{1,0:T(8,128)(2,1)}, f32[1,1024]{1,0:T(1,128)}, f32[1,256...) custom-call(bf16[4096,1024]{1,0:T(8,128)(2,1)S(1)} %get-tuple-elemen, ...), custom_call_target="tpu_custom_call" | custom-call | tf_op jit(solution)/shard_map/pallas_call | solution.py:488
  195.6 15.0 %shard_map.188.piece = bf16[1024,512]{1,0:T(8,128)(2,1)S(1)} custom-call(bf16[4096,1024]{1,0:T(8,128)(2,1)S(1)} %get-tuple-element.31.refs_0_.final, f32[1,1024]{1,0:T(1,128)S(1)} %get-tuple-element.42.after), custom_call_target="tpu_custom_call" | custom-call | tf_op jit(solution)/shard_map/pallas_call | solution.py:496
  210.6 1.0 shard_map.189

commit v4 on v3

--- a/solution.py
+++ b/solution.py
@@ -15,6 +15,7 @@
 AHEAD = 4
 HELD = 4, 8
 HEAD = 5, 16
+NEAR = 3
 MESH = pl.DeviceIdType.MESH
 
 
@@ -50,7 +51,8 @@
     finals, columns, serve, results = refs[11:14], refs[14:17], refs[17], refs[18:21]
     held = [refs[21:24], refs[24:27], refs[27:30]]
     gain, sums, in_sem, gain_sem, sum_send, sum_recv, send, recv = refs[30:38]
-    norm_send, norm_recv, wide_send, wide_recv, raw, top_sem, raw_send, raw_recv = refs[38:]
+    norm_send, norm_recv, wide_send, wide_recv, raw, top_sem, raw_send, raw_recv = refs[38:46]
+    own, serve_send, serve_recv = refs[46:]
     me, first, last = waits(n, site)
     late = lax.axis_index("site") == site - 1
     col = lax.axis_index("width")
@@ -74,14 +76,24 @@
         part = (pl.ds(0, top), pl.ds(0, chunks[0][2]))
         return pltpu.make_async_copy(inputs[0][k].at[part], held[0][k].at[part], top_sem.at[k])
 
+    near = [
+        jnp.logical_not((me < 2) & (lax.rem(me + p, n) >= NEAR)) for p in range(1, n)
+    ]
     for p in range(1, n):
-        pl.semaphore_signal(
-            barrier, inc=1, device_id={"rows": lax.rem(me + p, n)}, device_id_type=MESH
-        )
-    for p in range(1, wide):
-        pl.semaphore_signal(
-            barrier, inc=1, device_id={"width": lax.rem(col + p, wide)}, device_id_type=MESH
-        )
+        @pl.when(jnp.logical_not((me >= NEAR) & (lax.rem(me + p, n) < 2)))
+        def _(p=p):
+            pl.semaphore_signal(
+                barrier, inc=1, device_id={"rows": lax.rem(me + p, n)}, device_id_type=MESH
+            )
+
+    @pl.when(me == 0)
+    def _():
+        for p in range(1, wide):
+            pl.semaphore_signal(
+                barrier, inc=1, device_id={"width": lax.rem(col + p, wide)}, device_id_type=MESH
+            )
+
+    heard = jnp.where(me < 2, min(n, NEAR) - 1, n - 1) + jnp.where(me == 0, wide - 1, 0)
     ahead = min(AHEAD, len(chunks))
     for k in range(3):
         load_top(k).start()
@@ -124,11 +136,11 @@
             device_id={"rows": lax.rem(me + p, n)}, device_id_type=MESH,
         )
 
-    def norm_copy(p, slot):
-        return pltpu.make_async_remote_copy(
-            src_ref=serve.at[me, col], dst_ref=serve.at[slot, col],
-            send_sem=norm_send.at[p], recv_sem=norm_recv.at[p],
-            device_id={"rows": lax.rem(me + p, n)}, device_id_type=MESH,
+    def norm_copy(slot):
+        return pltpu.make_async_remote_copy(
+            src_ref=own, dst_ref=serve.at[slot, col],
+            send_sem=norm_send, recv_sem=norm_recv.at[slot],
+            device_id={"rows": 0}, device_id_type=MESH,
         )
 
     def wide_copy(p, slot):
@@ -136,6 +148,13 @@
             src_ref=serve.at[:, col], dst_ref=serve.at[:, slot],
             send_sem=wide_send.at[p], recv_sem=wide_recv.at[p],
             device_id={"width": lax.rem(col + p, wide)}, device_id_type=MESH,
+        )
+
+    def serve_copy(row):
+        return pltpu.make_async_remote_copy(
+            src_ref=serve, dst_ref=serve,
+            send_sem=serve_send.at[row], recv_sem=serve_recv,
+            device_id={"rows": row}, device_id_type=MESH,
         )
 
     has_next = (me < n - 1, me > 0)
@@ -161,11 +180,17 @@
             device_id={"rows": lax.rem(me + step[d] + n, n)}, device_id_type=MESH,
         )
 
-    def finish(j):
+    def finish(j, ready):
         a, c, cw = chunks[j]
         cols = pl.ds(c, cw)
         for p in range(1, n):
             sum_copy(j, p, lax.rem(me - p + n, n)).wait_recv()
+        if j == 0:
+            for p in range(1, n):
+                @pl.when(jnp.logical_not(near[p - 1]))
+                def _(p=p):
+                    for i in range(ready):
+                        sum_copy(i, p, me).start()
         total = sums[j, 0, :, pl.ds(0, cw)]
         for p in range(1, n):
             total = total + sums[j, p, :, pl.ds(0, cw)]
@@ -201,20 +226,30 @@
                 for k in range(3):
                     load_top(k).wait()
                 acc = rows_of(0, 0, top, acc)
-                pl.semaphore_wait(barrier, n + wide - 2)
+                pl.semaphore_wait(barrier, heard)
                 for d in (0, 1):
                     pl.when(opens[d])(raw_copy(d).start)
             update(ready, low, acc)
             for p in range(1, n):
-                sum_copy(ready, p, me).start()
+                send_sum = sum_copy(ready, p, me).start
+                if j == 0:
+                    pl.when(near[p - 1])(send_sum)
+                else:
+                    send_sum()
             ready += 1
-        finish(j)
+        finish(j, ready)
 
     for k in range(2):
         pltpu.make_async_copy(norms[k], gain.at[k], gain_sem.at[k]).wait()
-    serve[me, col] = (gain[0] + gain[1]).astype(jnp.bfloat16)
-    for p in range(1, n):
-        norm_copy(p, me).start()
+    own[...] = (gain[0] + gain[1]).astype(jnp.bfloat16)
+
+    @pl.when(me == 0)
+    def _():
+        serve[0, col] = own[...]
+
+    @pl.when(me > 0)
+    def _():
+        norm_copy(me).start()
 
     for d in (0, 1):
         @pl.when(opened[d])
@@ -309,20 +344,33 @@
             for j in range(len(chunks)):
                 for p in range(1, n):
                     sum_copy(j, p, me).wait_send()
-            for p in range(1, n):
-                norm_copy(p, me).wait_send()
-            for p in range(1, wide):
-                wide_copy(p, col).wait_send()
-                wide_copy(p, lax.rem(col - p + wide, wide)).wait_recv()
+
+            @pl.when(me > 0)
+            def _():
+                norm_copy(me).wait_send()
         relay(h)
         if h == 0:
-            for p in range(1, n):
-                norm_copy(p, lax.rem(me - p + n, n)).wait_recv()
-            for p in range(1, wide):
-                wide_copy(p, col).start()
+            @pl.when(me == 0)
+            def _():
+                for row in range(1, n):
+                    norm_copy(row).wait_recv()
+                for p in range(1, wide):
+                    wide_copy(p, col).start()
+                for p in range(1, wide):
+                    wide_copy(p, lax.rem(col - p + wide, wide)).wait_recv()
+                for row in range(1, n):
+                    serve_copy(row).start()
+                for p in range(1, wide):
+                    wide_copy(p, col).wait_send()
+                for row in range(1, n):
+                    serve_copy(row).wait_send()
         if h >= 1:
             drain(h - 1)
     drain(n - 2)
+
+    @pl.when(me > 0)
+    def _():
+        serve_copy(0).wait_recv()
 
 
 def store(n, site, kept, *refs):
@@ -469,7 +517,7 @@
                 dma((count, n)),
                 dma((2, n - 1, count)),
                 dma((2, n - 1, count)),
-                dma((n,)),
+                dma,
                 dma((n,)),
                 dma((wide,)),
                 dma((wide,)),
@@ -477,6 +525,9 @@
                 dma((3,)),
                 dma((2,)),
                 dma((2,)),
+                vmem((part // lanes, lanes), jnp.bfloat16),
+                dma((n,)),
+                dma,
             ],
             compiler_params=pltpu.CompilerParams(
                 collective_id=0,

time: 212 us -> 211 us (level)
  no operation moved by 1% of the time
where the time goes in v4:
time: 211 us
  Pallas kernels  210 us (100%)
    pallas_call x1, Pallas kernels, per_device(): pl.pallas_call(functools.partial(gather, n, wide, site, chunks), out_shap...  188 us
    pallas_call x1, Pallas kernels, per_device(): pl.pallas_call(functools.partial(finish_gather, n, site), out_shape=vmem(...  14.9 us
    pallas_call x1, Pallas kernels, per_device(): pl.pallas_call(functools.partial(store, n, site, kept), out_shape=[shaped...  6.31 us

profile of v4, /device:TPU:1, one launch (start us, length us, event | category | flops | bytes accessed | tf_op | source)
XLA Modules:
  0.0 210.8 jit_solution(11821169728685955802)
XLA Ops:
  0.6 188.0 %shard_map.186 = (bf16[4096,1024]{1,0:T(8,128)(2,1)S(1)}, bf16[4096,256]{1,0:T(8,128)(2,1)S(1)}, bf16[4096,256]{1,0:T(8,128)(2,1)S(1)}, f32[1,1024]{1,0:T(1,128)...) custom-call(f32[1024,1024]{1,0:T(8,128)} %refs_0_.1, ...), custom_call_target="tpu_custom_call" | custom-call | tf_op jit(solution)/shard_map/pallas_call | solution.py:505
  188.6 6.3 %shard_map.187 = (bf16[4096,1024]{1,0:T(8,128)(2,1)}, bf16[4096,256]{1,0:T(8,128)(2,1)}, bf16[4096,256]{1,0:T(8,128)(2,1)}, f32[1,1024]{1,0:T(1,128)}, f32[1,256...) custom-call(bf16[4096,1024]{1,0:T(8,128)(2,1)S(1)} %get-tuple-elemen, ...), custom_call_target="tpu_custom_call" | custom-call | tf_op jit(solution)/shard_map/pallas_call | solution.py:539
  195.0 14.9 %shard_map.188.piece = bf16[1024,512]{1,0:T(8,128)(2,1)S(1)} custom-call(bf16[4096,1024]{1,0:T(8,128)(2,1)S(1)} %get-tuple-element.31.refs_0_.final, f32[1,1024]{1,0:T(1,128)S(1)} %get-tuple-element.42.after), custom_call_target="tpu_custom_call" | custom-call | tf_op jit(solution)/shard_map/pallas_call | solution.py:547
  209.8 1.0 shard_map.189

commit v5 on v4

--- a/solution.py
+++ b/solution.py
@@ -76,11 +76,15 @@
         part = (pl.ds(0, top), pl.ds(0, chunks[0][2]))
         return pltpu.make_async_copy(inputs[0][k].at[part], held[0][k].at[part], top_sem.at[k])
 
+    for k in range(3):
+        load_top(k).start()
     near = [
-        jnp.logical_not((me < 2) & (lax.rem(me + p, n) >= NEAR)) for p in range(1, n)
+        jnp.logical_not((me < 2) & (lax.rem(me + p, n) >= NEAR - me)) for p in range(1, n)
     ]
     for p in range(1, n):
-        @pl.when(jnp.logical_not((me >= NEAR) & (lax.rem(me + p, n) < 2)))
+        to = lax.rem(me + p, n)
+
+        @pl.when(jnp.logical_not((to < 2) & (me >= NEAR - to)))
         def _(p=p):
             pl.semaphore_signal(
                 barrier, inc=1, device_id={"rows": lax.rem(me + p, n)}, device_id_type=MESH
@@ -93,10 +97,8 @@
                 barrier, inc=1, device_id={"width": lax.rem(col + p, wide)}, device_id_type=MESH
             )
 
-    heard = jnp.where(me < 2, min(n, NEAR) - 1, n - 1) + jnp.where(me == 0, wide - 1, 0)
+    heard = jnp.where(me == 0, min(n, NEAR) - 1, jnp.where(me == 1, 1, n - 1)) + jnp.where(me == 0, wide - 1, 0)
     ahead = min(AHEAD, len(chunks))
-    for k in range(3):
-        load_top(k).start()
     for j in range(ahead):
         for k in range(3):
             load(j, k).start()

time: 211 us -> 211 us (level)
  no operation moved by 1% of the time
where the time goes in v5:
time: 211 us
  Pallas kernels  210 us (100%)
    pallas_call x1, Pallas kernels, per_device(): pl.pallas_call(functools.partial(gather, n, wide, site, chunks), out_shap...  188 us
    pallas_call x1, Pallas kernels, per_device(): pl.pallas_call(functools.partial(finish_gather, n, site), out_shape=vmem(...  14.9 us
    pallas_call x1, Pallas kernels, per_device(): pl.pallas_call(functools.partial(store, n, site, kept), out_shape=[shaped...  6.31 us

profile of v5, /device:TPU:1, one launch (start us, length us, event | category | flops | bytes accessed | tf_op | source)
XLA Modules:
  0.0 210.8 jit_solution(13228468753095512956)
XLA Ops:
  0.6 188.0 %shard_map.186 = (bf16[4096,1024]{1,0:T(8,128)(2,1)S(1)}, bf16[4096,256]{1,0:T(8,128)(2,1)S(1)}, bf16[4096,256]{1,0:T(8,128)(2,1)S(1)}, f32[1,1024]{1,0:T(1,128)...) custom-call(f32[1024,1024]{1,0:T(8,128)} %refs_0_.1, ...), custom_call_target="tpu_custom_call" | custom-call | tf_op jit(solution)/shard_map/pallas_call | solution.py:507
  188.6 6.3 %shard_map.187 = (bf16[4096,1024]{1,0:T(8,128)(2,1)}, bf16[4096,256]{1,0:T(8,128)(2,1)}, bf16[4096,256]{1,0:T(8,128)(2,1)}, f32[1,1024]{1,0:T(1,128)}, f32[1,256...) custom-call(bf16[4096,1024]{1,0:T(8,128)(2,1)S(1)} %get-tuple-elemen, ...), custom_call_target="tpu_custom_call" | custom-call | tf_op jit(solution)/shard_map/pallas_call | solution.py:541
  194.9 14.9 %shard_map.188.piece = bf16[1024,512]{1,0:T(8,128)(2,1)S(1)} custom-call(bf16[4096,1024]{1,0:T(8,128)(2,1)S(1)} %get-tuple-element.31.refs_0_.final, f32[1,1024]{1,0:T(1,128)S(1)} %get-tuple-element.42.after), custom_call_target="tpu_custom_call" | custom-call | tf_op jit(solution)/shard_map/pallas_call | solution.py:549
  209.8 1.0 shard_map.189

commit v6 on v4

--- a/solution.py
+++ b/solution.py
@@ -14,7 +14,7 @@
 LEAD = 4
 AHEAD = 4
 HELD = 4, 8
-HEAD = 5, 16
+HEAD = 6, 16
 NEAR = 3
 MESH = pl.DeviceIdType.MESH
 
@@ -37,7 +37,7 @@
 
 
 def block_of(depth):
-    return min(depth, 64)
+    return min(depth, 128)
 
 
 def waits(n, site):

time: 211 us -> 211 us (level)
  no operation moved by 1% of the time
where the time goes in v6:
time: 211 us
  Pallas kernels  210 us (100%)
    pallas_call x1, Pallas kernels, per_device(): pl.pallas_call(functools.partial(gather, n, wide, site, chunks), out_shap...  189 us
    pallas_call x1, Pallas kernels, per_device(): pl.pallas_call(functools.partial(finish_gather, n, site), out_shape=vmem(...  14.3 us
    pallas_call x1, Pallas kernels, per_device(): pl.pallas_call(functools.partial(store, n, site, kept), out_shape=[shaped...  6.31 us

profile of v6, /device:TPU:1, one launch (start us, length us, event | category | flops | bytes accessed | tf_op | source)
XLA Modules:
  0.0 211.0 jit_solution(7048392825023422928)
XLA Ops:
  0.6 188.7 %shard_map.186 = (bf16[4096,1024]{1,0:T(8,128)(2,1)S(1)}, bf16[4096,256]{1,0:T(8,128)(2,1)S(1)}, bf16[4096,256]{1,0:T(8,128)(2,1)S(1)}, f32[1,1024]{1,0:T(1,128)...) custom-call(f32[1024,1024]{1,0:T(8,128)} %refs_0_.1, ...), custom_call_target="tpu_custom_call" | custom-call | tf_op jit(solution)/shard_map/pallas_call | solution.py:505
  189.4 6.3 %shard_map.187 = (bf16[4096,1024]{1,0:T(8,128)(2,1)}, bf16[4096,256]{1,0:T(8,128)(2,1)}, bf16[4096,256]{1,0:T(8,128)(2,1)}, f32[1,1024]{1,0:T(1,128)}, f32[1,256...) custom-call(bf16[4096,1024]{1,0:T(8,128)(2,1)S(1)} %get-tuple-elemen, ...), custom_call_target="tpu_custom_call" | custom-call | tf_op jit(solution)/shard_map/pallas_call | solution.py:539
  195.7 14.3 %shard_map.188.piece = bf16[1024,512]{1,0:T(8,128)(2,1)S(1)} custom-call(bf16[4096,1024]{1,0:T(8,128)(2,1)S(1)} %get-tuple-element.31.refs_0_.final, f32[1,1024]{1,0:T(1,128)S(1)} %get-tuple-element.42.after), custom_call_target="tpu_custom_call" | custom-call | tf_op jit(solution)/shard_map/pallas_call | solution.py:547
  210.0 1.0 shard_map.189
